TPU v7x, 32 devices: a whole 2x2x4 slice. The times are simulated.
32 devices in a mesh: expert: 8 (over y, x, core), tensor: 4 (over z).
Axes of the slice: x: 2, y: 2, z: 4, core: 2. Of those that a mesh axis runs over, the one named last changes fastest.
Arguments:
- tokens: bfloat16 [1024, 2560], P('expert', 'tensor'), may hold values from -6 to 6
- slot: int32 [1024, 1], P('expert'), may hold values from 0 to 15; in each aligned block of 128 rows (0 to 127, 128 to 255, ...) at most 16 rows name the same one
- mask: int32 [1024], P('expert'), may hold values 0 or 1
- hot_group: int32 [1], replicated, may hold values from 0 to 7
- router_weight: bfloat16 [2560, 8], replicated, may hold values from -0.125 to 0.125
- exp_gate: bfloat16 [8, 2560, 4096], P('expert', None, 'tensor'), may hold values from -0.125 to 0.125
- exp_up: bfloat16 [8, 2560, 4096], P('expert', None, 'tensor'), may hold values from -0.125 to 0.125
- exp_down: bfloat16 [8, 4096, 2560], P('expert', 'tensor'), may hold values from -0.09375 to 0.09375
- sh_gate: bfloat16 [2560, 4096], P('expert', 'tensor'), may hold values from -0.125 to 0.125
- sh_up: bfloat16 [2560, 4096], P('expert', 'tensor'), may hold values from -0.125 to 0.125
- sh_down: bfloat16 [4096, 2560], P('tensor', 'expert'), may hold values from -0.09375 to 0.09375
Outputs:
- mixed: bfloat16 [1024, 2560], P('expert', 'tensor')
Inputs may be any that keep to these rules, and one draw needn't show every extreme that they name: Slot 2 g is the home slot of expert g, slot 2 g + 1 the spare slot of group g. Among the 128 tokens of one group no slot is named by more than 16 tokens, a bound that some block reaches.
All inputs are finite; a program needn't handle non-finite values. No bound on the sum of `mask` on one device may be relied on, other than what follows from the above.
Results may differ from a plain program's by a relative error of at most 0.0052.
Values may be sent and summed in bfloat16 or wider, within the bound.
No kernel may reach another device: no remote copies, remote signals or barrier semaphores. Data moves between devices by JAX's collectives and lax.ppermute only.
A program may use at most 192 MiB of HBM per device.

v0:
```python
import jax
import jax.numpy as jnp
from jax import lax
from jax.sharding import PartitionSpec as P


def from_root(block, axis, source):
    block = jnp.where(lax.axis_index(axis) == source, block, jnp.zeros_like(block))
    return lax.psum(block, axis)


def expert_ffn(batch_rows, w_gate, w_up, w_down):
    gated = jnp.dot(batch_rows, w_gate, preferred_element_type=jnp.float32)
    upward = jnp.dot(batch_rows, w_up, preferred_element_type=jnp.float32)
    hidden = (jax.nn.silu(gated) * upward).astype(jnp.bfloat16)
    return jnp.dot(hidden, w_down, preferred_element_type=jnp.float32)


def local(
    tokens,
    slot,
    mask,
    hot_group,
    router_weight,
    exp_gate,
    exp_up,
    exp_down,
    sh_gate,
    sh_up,
    sh_down,
):
    n_groups = lax.axis_size("expert")
    whole = lax.all_gather(tokens, "tensor", axis=1, tiled=True)
    tok_count = whole.shape[0]
    width = whole.shape[1]
    capacity = tok_count // n_groups
    slot_count = 2 * n_groups
    slot_ids = slot[:, 0]
    hot_index = hot_group[0]
    expert_id = jnp.where(slot_ids % 2 == 0, slot_ids // 2, hot_index)
    logits = jnp.dot(whole, router_weight, preferred_element_type=jnp.float32)
    chosen = expert_id[:, None] == lax.broadcasted_iota(jnp.int32, (1, router_weight.shape[1]), 1)
    weighting = jax.nn.sigmoid(jnp.sum(jnp.where(chosen, logits, 0.0), axis=1))
    shared_gate = jnp.dot(
        whole,
        lax.all_gather(sh_gate, "expert", axis=0, tiled=True),
        preferred_element_type=jnp.float32,
    )
    shared_up = jnp.dot(
        whole,
        lax.all_gather(sh_up, "expert", axis=0, tiled=True),
        preferred_element_type=jnp.float32,
    )
    sh_hidden = (jax.nn.silu(shared_gate) * shared_up).astype(jnp.bfloat16)
    shared_terms = jnp.dot(
        sh_hidden,
        lax.all_gather(sh_down, "expert", axis=1, tiled=True),
        preferred_element_type=jnp.float32,
    )
    shared = lax.psum_scatter(shared_terms, "tensor", scatter_dimension=1, tiled=True)
    slot_hits = (slot_ids[:, None] == lax.broadcasted_iota(jnp.int32, (1, slot_count), 1)).astype(
        jnp.int32
    )
    position = jnp.sum((jnp.cumsum(slot_hits, axis=0) - 1) * slot_hits, axis=1)
    target = slot_ids * capacity + position
    placing = (
        lax.broadcasted_iota(jnp.int32, (slot_count * capacity, 1), 0) == target[None, :]
    ).astype(jnp.bfloat16)
    outgoing = jnp.dot(placing, tokens, preferred_element_type=jnp.float32).astype(jnp.bfloat16)
    quarter = lax.all_to_all(outgoing, "expert", split_axis=0, concat_axis=0, tiled=True)
    arrived = lax.all_gather(quarter, "tensor", axis=1, tiled=True)
    replica = (
        from_root(exp_gate[0], "expert", hot_index),
        from_root(exp_up[0], "expert", hot_index),
        from_root(exp_down[0], "expert", hot_index),
    )
    grouped = arrived.reshape(n_groups, 2, capacity, width)
    home_rows = grouped[:, 0].reshape(n_groups * capacity, width)
    spare_rows = grouped[:, 1].reshape(n_groups * capacity, width)
    home_part = expert_ffn(home_rows, exp_gate[0], exp_up[0], exp_down[0])
    spare_part = expert_ffn(spare_rows, replica[0], replica[1], replica[2])
    partials = jnp.stack(
        [
            home_part.reshape(n_groups, capacity, width),
            spare_part.reshape(n_groups, capacity, width),
        ],
        axis=1,
    )
    partials = partials.reshape(slot_count * capacity, width)
    summed = lax.psum_scatter(partials, "tensor", scatter_dimension=1, tiled=True).astype(
        jnp.bfloat16
    )
    returned = lax.all_to_all(summed, "expert", split_axis=0, concat_axis=0, tiled=True)
    routed = lax.dot_general(
        placing, returned, (((0,), (0,)), ((), ())), preferred_element_type=jnp.float32
    )
    keep_rows = mask.astype(jnp.float32)
    mixed = keep_rows[:, None] * (shared + weighting[:, None] * routed)
    return mixed.astype(jnp.bfloat16)


def solution(mesh):
    in_specs = (
        P("expert", "tensor"),
        P("expert", None),
        P("expert"),
        P(),
        P(),
        P("expert", None, "tensor"),
        P("expert", None, "tensor"),
        P("expert", "tensor", None),
        P("expert", "tensor"),
        P("expert", "tensor"),
        P("tensor", "expert"),
    )
    out_specs = P("expert", "tensor")
    return jax.shard_map(local, mesh=mesh, in_specs=in_specs, out_specs=out_specs, check_vma=False)
```

profile of v0, /device:TPU:0, one launch (start us, length us, event | category | flops | bytes accessed | tf_op | source)
XLA Modules:
  0.0 397.9 jit_solution(10795923195216460951)
XLA Ops:
  7.4 0.7 fusion.37
  8.1 0.2 reduce_window_sum.11
  8.3 0.8 select_reduce_fusion
  9.1 0.7 multiply_add_fusion
  9.8 1.9 convolution_convert_fusion
  11.7 5.2 %all-to-all-start = ((bf16[8,32,640]{2,1,0:T(8,128)(2,1)}), bf16[8,32,640]{2,1,0:T(8,128)(2,1)S(1)}, u32[]{:S(2)}, u32[]{:S(2)}) async-start(bf16[8,32,640]{2,1,0:T(8,128)(2,1)} %bitcast.3), calls=%async_computation.1 | async-start | bytes 655360 | tf_op jit(solution)/shard_map/all_to_all | solution.py:70
  16.9 0.0 all-gather.11.cloned.1.call-start
  17.6 6.9 %all-to-all-done = bf16[8,32,640]{2,1,0:T(8,128)(2,1)S(1)} async-done(((bf16[8,32,640]{2,1,0:T(8,128)(2,1)}), bf16[8,32,640]{2,1,0:T(8,128)(2,1)S(1)}, u32[]{:S(2)}, u32[]{:S(2)}) %all-to-all-start) | async-done | bytes 327712 | tf_op jit(solution)/shard_map/all_to_all | solution.py:70
  24.5 0.7 copy-done.1
  25.2 0.0 all-gather.11.cloned.1.call-update
  25.2 0.0 all-reduce.3.cloned.1.call-start
  25.3 5.1 %bitcast_select_fusion = bf16[1024,2560]{1,0:T(8,128)(2,1)} fusion(bf16[1,1024,2560]{2,1,0:T(8,128)(2,1)} %param.18, pred[]{:T(512)S(6)} %eq.64), kind=kLoop, calls=%fused_computation.2 | loop fusion | flops 2621440 | bytes 10485761 | tf_op jit(solution)/shard_map/jit(_where)/select_n | solution.py:8
  30.4 9.0 %bitcast_select_fusion.1 = (bf16[2560,1024]{1,0:T(8,128)(2,1)}, bf16[2560,1024]{1,0:T(8,128)(2,1)}) fusion(bf16[1,2560,1024]{2,1,0:T(8,128)(2,1)} %param.17, pred[]{:T(512)S(6)} %eq.64, bf16[1,2560,1024]{2,1,0:T(8,128)(2,1)} %param.16), kind=kLoop, calls=%fused_computation.3 | loop fusion | flops 5242880 | bytes 20971520 | tf_op jit(solution)/shard_map/jit(_where)/select_n | solution.py:8
  39.4 0.0 all-reduce.3.cloned.1.call-update
  39.4 0.0 all-gather.5.cloned.1.call-start
  39.5 0.7 all-gather.5.cloned.1.call-update
  40.2 0.0 all-gather.7.cloned.1.call-start
  40.2 0.7 all-gather.7.cloned.1.call-update
  40.9 0.0 all-gather.9.cloned.1.call-start
  40.9 0.5 all-gather.9.cloned.1.call-update
  41.5 0.0 reduce-scatter.5.cloned.1.call-start
  41.5 15.5 %all-gather.11.cloned.1.call-done = bf16[256,2560]{1,0:T(8,128)(2,1)} async-done(((bf16[256,640]{1,0:T(8,128)(2,1)}), bf16[256,2560]{1,0:T(8,128)(2,1)}) %all-gather.11.cloned.1.call-update) | async-done | bytes 1310736 | tf_op jit(solution)/shard_map/all_gather | solution.py:71
  57.1 1.4 fusion.41
  58.4 0.0 slice-start
  58.5 3.7 fusion.4
  62.1 0.0 slice-start.1
  62.1 3.7 fusion.12
  65.9 0.9 fusion.6
  66.7 217.1 %all-reduce.3.cloned.1.call-done = (bf16[1024,2560]{1,0:T(8,128)(2,1)}, bf16[2560,1024]{1,0:T(8,128)(2,1)}, bf16[2560,1024]{1,0:T(8,128)(2,1)}) async-done(((bf16[1024,2560]{1,0:T(8,128)(2,1)}, bf16[2560,1024]{1,0:T(8,128)(2,1)}, bf16[2560,1024]{1,0:T(8,128)(2,1)}), (bf16[1024,2560]{1,0:T(8,128)(2,1)}, bf16[2560,1024]{1,0:T(8,128)(2,1)}, bf16[2560,1024]{1,0:T(8,128)(2,1)})) %all-reduce.3.cloned.1.call-update) | async-done | bytes 15728656 | tf_op jit(solution)/shard_map/psum | solution.py:9
  283.9 4.1 %fusion.43 = f32[128,1024]{1,0:T(8,128)} fusion(bf16[128,2560]{1,0:T(8,128)(2,1)S(1)} %bitcast.58, bf16[2560,1024]{1,0:T(8,128)(2,1)} %get-tuple-element.7), kind=kOutput, calls=%fused_computation.58 | convolution fusion | flops 671088640 | bytes 6422528 | tf_op jit(solution)/shard_map/dot_general | solution.py:13
  288.0 5.8 %fusion.21 = f32[128,2560]{1,0:T(8,128)S(1)} fusion(bf16[1024,2560]{1,0:T(8,128)(2,1)} %get-tuple-element.5, bf16[128,2560]{1,0:T(8,128)(2,1)S(1)} %bitcast.59, bf16[2560,1024]{1,0:T(8,128)(2,1)} %get-tuple-element.6, f32[128,1024]{1,0:T(8,128)} %fusion.43), kind=kOutput, calls=%fused_computation.24 | convolution fusion | flops 1342963712 | bytes 12976128 | tf_op jit(solution)/shard_map/dot_general | solution.py:16
  293.8 0.2 pad_maximum_fusion
  294.0 0.0 copy-start.2
  294.0 1.7 copy.12
  295.7 0.0 reduce-scatter.5.cloned.1.call-update
  295.7 0.0 reduce-scatter.3.cloned.1.call-start
  295.8 24.9 %all_gather.15 = bf16[128,2560]{1,0:T(8,128)(2,1)S(1)} all-gather(bf16[128,640]{1,0:T(8,128)(2,1)S(1)} %copy-done.2), channel_id=1, replica_groups=mesh['expert'=8,'tensor'=4] {'tensor'}, dimensions={1}, use_global_device_ids=true | all-gather | bytes 819200 | tf_op jit(solution)/shard_map/all_gather | solution.py:33
  320.7 3.4 fusion.42
  324.1 0.0 all-gather.7.cloned.1.call-done
  324.1 0.0 all-gather.9.cloned.1.call-done
  324.1 7.8 %fusion.22 = f32[128,2560]{1,0:T(8,128)} fusion(bf16[1024,2560]{0,1:T(8,128)(2,1)} %all-gather.9.cloned.1.call-done, bf16[128,2560]{1,0:T(8,128)(2,1)S(1)} %all_gather.15, bf16[2560,1024]{1,0:T(8,128)(2,1)} %all-gather.7.cloned.1.call-done, f32[128,1024]{1,0:T(8,128)S(1)} %fusion.42), kind=kOutput, calls=%fused_computation.25 | convolution fusion | flops 1342963712 | bytes 12976128 | tf_op jit(solution)/shard_map/dot_general | solution.py:55
  331.9 0.0 reduce-scatter.3.cloned.1.call-update
  331.9 22.1 %reduce-scatter.5.cloned.1.call-done = f32[256,640]{1,0:T(8,128)} async-done(((f32[256,2560]{1,0:T(8,128)}), f32[256,640]{1,0:T(8,128)}) %reduce-scatter.5.cloned.1.call-update) | async-done | bytes 655376 | tf_op jit(solution)/shard_map/reduce_scatter | solution.py:90
  354.0 1.8 convert_element_type.31
  355.8 3.5 all-to-all-start.1
  359.3 0.3 fusion.20
  359.6 28.9 %reduce-scatter.3.cloned.1.call-done = f32[128,640]{1,0:T(8,128)} async-done(((f32[128,2560]{1,0:T(8,128)}), f32[128,640]{1,0:T(8,128)}) %reduce-scatter.3.cloned.1.call-update) | async-done | bytes 327696 | tf_op jit(solution)/shard_map/reduce_scatter | solution.py:60
  388.5 1.9 fusion.19
  (16 shorter events, 0.1 us)
Async XLA Ops:
  7.4 351.9 %copy-start = (bf16[2560,8]{0,1:T(8,128)(2,1)S(1)}, bf16[2560,8]{0,1:T(8,128)(2,1)}, u32[]{:S(2)}) copy-start(bf16[2560,8]{0,1:T(8,128)(2,1)} %param.15) | copy-start | bytes 122884
  11.7 12.8 %all-to-all-start = ((bf16[8,32,640]{2,1,0:T(8,128)(2,1)}), bf16[8,32,640]{2,1,0:T(8,128)(2,1)S(1)}, u32[]{:S(2)}, u32[]{:S(2)}) async-start(bf16[8,32,640]{2,1,0:T(8,128)(2,1)} %bitcast.3), calls=%async_computation.1 | async-start | bytes 655360 | tf_op jit(solution)/shard_map/all_to_all | solution.py:70
  16.9 40.2 %all-gather.11.cloned.1.call-start = ((), (), s32[]{:S(2)}) async-start(), calls=%async_computation.8 | async-start | bytes 1638400 | tf_op jit(solution)/shard_map/all_gather | solution.py:71
  24.5 0.7 copy-start.1
  25.2 258.6 %all-reduce.3.cloned.1.call-start = ((), (), s32[]{:S(2)}) async-start(), calls=%async_computation.10 | async-start | bytes 31457280 | tf_op jit(solution)/shard_map/psum | solution.py:9
  39.4 281.2 %all-gather.5.cloned.1.call-start = ((), (), s32[]{:S(2)}) async-start(), calls=%async_computation.4 | async-start | bytes 5898240 | tf_op jit(solution)/shard_map/all_gather | solution.py:46
  40.2 283.9 %all-gather.7.cloned.1.call-start = ((), (), s32[]{:S(2)}) async-start(), calls=%async_computation.5 | async-start | bytes 5898240 | tf_op jit(solution)/shard_map/all_gather | solution.py:51
  40.9 283.2 %all-gather.9.cloned.1.call-start = ((), (), s32[]{:S(2)}) async-start(), calls=%async_computation.6 | async-start | bytes 5898240 | tf_op jit(solution)/shard_map/all_gather | solution.py:57
  41.5 312.5 %reduce-scatter.5.cloned.1.call-start = ((), (), s32[]{:S(2)}) async-start(), calls=%async_computation.9 | async-start | bytes 3276800 | tf_op jit(solution)/shard_map/reduce_scatter | solution.py:90
  58.4 7.4 %slice-start = ((s8[5242880]{0:T(1024)(128)(4,1)}), s8[4194304]{0:T(1024)(128)(4,1)S(1)}, s32[]{:S(2)}) async-start(s8[5242880]{0:T(1024)(128)(4,1)} %bitcast.55), calls=%async_computation.11 | async-start | bytes 8388608
  62.1 3.7 slice-start.1
  294.0 1.8 copy-start.2
  295.7 92.8 %reduce-scatter.3.cloned.1.call-start = ((), (), s32[]{:S(2)}) async-start(), calls=%async_computation.7 | async-start | bytes 1638400 | tf_op jit(solution)/shard_map/reduce_scatter | solution.py:60
  324.0 7.9 %copy-start.3 = (s32[128,1]{0,1:T(1,128)S(1)}, s32[128,1]{0,1:T(1,128)}, u32[]{:S(2)}) copy-start(s32[128,1]{0,1:T(1,128)} %param.12) | copy-start | bytes 1540
  324.0 35.5 %copy-start.4 = (s32[128]{0:T(128)S(1)}, s32[128]{0:T(128)}, u32[]{:S(2)}) copy-start(s32[128]{0:T(128)} %param.13) | copy-start | bytes 1540
  355.8 32.7 %all-to-all-start.1 = ((bf16[8,32,640]{2,1,0:T(8,128)(2,1)}), bf16[8,32,640]{2,1,0:T(8,128)(2,1)S(1)}, u32[]{:S(2)}, u32[]{:S(2)}) async-start(bf16[8,32,640]{2,1,0:T(8,128)(2,1)} %bitcast.16), calls=%async_computation.3 | async-start | bytes 655360 | tf_op jit(solution)/shard_map/all_to_all | solution.py:93
Sparse Core Ops, SparseCore 0:
  25.4 31.6 all-gather.10
  58.9 54.3 all-gather.4
  115.2 62.2 all-gather.6
  179.2 57.2 all-gather.8
  295.9 58.0 reduce-scatter.4
  356.1 32.3 reduce-scatter.2
Sparse Core Ops, SparseCore 1:
  39.5 244.3 all-reduce.2
where the time goes:
time: 398 us
  waiting for transfers between devices  293 us (74%)
  matrix products  33.4 us (8%)
  blocking collectives  24.9 us (6%)
  other arithmetic  18.6 us (5%)
  between operations  15.8 us (4%)
  starting transfers between devices  8.93 us (2%)
    psum x1, waiting for transfers between devices, from_root(): return lax.psum(block, axis)  217 us
    reduce_scatter x1, waiting for transfers between devices, local(): lax.psum_scatter(shared_terms, 'tensor', scatter_dimension=1, tiled=True)  28.9 us
    all_gather x1, blocking collectives, local(): whole = lax.all_gather(tokens, 'tensor', axis=1, tiled=True)  24.9 us
    reduce_scatter x1, waiting for transfers between devices, local(): lax.psum_scatter(partials, 'tensor', scatter_dimension=1, tiled=True)  22.1 us
    all_gather x1, waiting for transfers between devices, local(): arrived = lax.all_gather(quarter, 'tensor', axis=1, tiled=True)  15.5 us
    select_n x2, other arithmetic, from_root(): jnp.where(lax.axis_index(axis) == source, block, jnp.zeros_like(block))  14.1 us
  transfers between devices with their start and end apart: 9, of which 5 were waited for; matrix products, arithmetic and copies ran while one was open for 12% of the time, Pallas kernels for 0%

commit v1 on v0

--- a/solution.py
+++ b/solution.py
@@ -6,7 +6,7 @@
 
 def from_root(block, axis, source):
     block = jnp.where(lax.axis_index(axis) == source, block, jnp.zeros_like(block))
-    return lax.psum(block, axis)
+    return jnp.sum(lax.all_gather(block, axis), axis=0)
 
 
 def expert_ffn(batch_rows, w_gate, w_up, w_down):

time: 398 us -> 876 us (2.20)
  waiting for transfers between devices: 293 us -> 724 us
  other arithmetic: 18.6 us -> 72.3 us
    all_gather x0 -> x3, waiting for transfers between devices: none -> 547 us  [from_root(): return jnp.sum(lax.all_gather(block, axis), axis=0)]
    psum x1 -> x0, waiting for transfers between devices: 217 us -> none  [from_root(): return lax.psum(block, axis)]
    reduce_sum x0 -> x3, other arithmetic: none -> 59.8 us  [from_root(): return jnp.sum(lax.all_gather(block, axis), axis=0)]
    all_gather x1, waiting for transfers between devices: 0.02 us -> 42.9 us  [local(): lax.all_gather(sh_down, 'expert', axis=1, tiled=True)]
    all_gather x1, waiting for transfers between devices: 0.02 us -> 37 us  [local(): lax.all_gather(sh_up, 'expert', axis=0, tiled=True)]
    reduce_scatter x1, waiting for transfers between devices: 22.1 us -> 46.8 us  [local(): lax.psum_scatter(partials, 'tensor', scatter_dimension=1, tiled=True)]
    all_to_all x0 -> x1, blocking collectives: none -> 12.7 us  [local(): lax.all_to_all(outgoing, 'expert', split_axis=0, concat_axis=0, tiled=True)]
  transfers between devices with their start and end apart: 9 -> 10, of which waited for: 5 -> 8; matrix products, arithmetic and copies ran while one was open for 12% -> 11% of each run, Pallas kernels for 0% -> 0%
where the time goes in v1:
time: 876 us; the launch traced here: 875 us
  waiting for transfers between devices  724 us (83%)
  other arithmetic  72.3 us (8%)
  blocking collectives  31.1 us (4%)
  matrix products  25.2 us (3%)
  between operations  14.1 us (2%)
    all_gather x3, waiting for transfers between devices, from_root(): return jnp.sum(lax.all_gather(block, axis), axis=0)  547 us
    reduce_sum x3, other arithmetic, from_root(): return jnp.sum(lax.all_gather(block, axis), axis=0)  59.8 us
    reduce_scatter x1, waiting for transfers between devices, local(): lax.psum_scatter(partials, 'tensor', scatter_dimension=1, tiled=True)  46.8 us
    all_gather x1, waiting for transfers between devices, local(): lax.all_gather(sh_down, 'expert', axis=1, tiled=True)  42.9 us
    all_gather x1, waiting for transfers between devices, local(): lax.all_gather(sh_up, 'expert', axis=0, tiled=True)  37 us
    reduce_scatter x1, waiting for transfers between devices, local(): lax.psum_scatter(shared_terms, 'tensor', scatter_dimension=1, tiled=True)  27.5 us
    all_gather x1, waiting for transfers between devices, local(): arrived = lax.all_gather(quarter, 'tensor', axis=1, tiled=True)  21 us
    all_gather x1, blocking collectives, local(): whole = lax.all_gather(tokens, 'tensor', axis=1, tiled=True)  18.3 us
  transfers between devices with their start and end apart: 10, of which 8 were waited for; matrix products, arithmetic and copies ran while one was open for 11% of the time, Pallas kernels for 0%

profile of v1, /device:TPU:0, one launch (start us, length us, event | category | flops | bytes accessed | tf_op | source)
XLA Modules:
  0.0 875.4 jit_solution(442983896324345497)
XLA Ops:
  6.5 0.7 fusion.35
  7.3 0.2 reduce_window_sum.11
  7.5 0.8 select_reduce_fusion
  8.3 0.7 multiply_add_fusion
  9.0 1.1 convolution_convert_fusion
  10.1 12.7 %all_to_all.24 = bf16[8,32,640]{2,1,0:T(8,128)(2,1)} all-to-all(bf16[8,32,640]{2,1,0:T(8,128)(2,1)S(1)} %bitcast.73), channel_id=1, replica_groups=mesh['expert'=8,'tensor'=4] {'expert'}, dimensions={0} | all-to-all | bytes 655360 | tf_op jit(solution)/shard_map/all_to_all | solution.py:70
  22.9 0.0 all-gather.16.cloned.1.call-start
  23.6 2.7 broadcast_select_fusion.2
  26.3 0.0 all-gather.18.cloned.1.call-start
  26.3 2.6 broadcast_select_fusion.1
  29.0 0.0 all-gather.20.cloned.1.call-start
  29.0 2.6 broadcast_select_fusion
  31.7 0.0 all-gather.8.cloned.1.call-start
  31.7 0.5 all-gather.8.cloned.1.call-update
  32.3 0.5 all-gather.10.cloned.1.call-update
  32.9 0.7 all-gather.12.cloned.1.call-update
  33.6 21.0 %all-gather.14.cloned.1.call-done = bf16[256,2560]{1,0:T(8,128)(2,1)} async-done(((bf16[256,640]{1,0:T(8,128)(2,1)}), bf16[256,2560]{1,0:T(8,128)(2,1)}) %all-gather.14.cloned.1.call-update) | async-done | bytes 1310736 | tf_op jit(solution)/shard_map/all_gather | solution.py:71
  54.7 1.5 fusion.38
  56.2 3.6 fusion.6
  59.8 1.0 fusion.17
  60.9 0.3 slice-done.3
  61.2 0.9 fusion.8
  62.0 190.9 %all-gather.16.cloned.1.call-done = bf16[8,2560,1024]{2,1,0:T(8,128)(2,1)} async-done(((bf16[1,2560,1024]{2,1,0:T(8,128)(2,1)}), bf16[8,2560,1024]{2,1,0:T(8,128)(2,1)}) %all-gather.16.cloned.1.call-update) | async-done | bytes 41943056 | tf_op jit(solution)/shard_map/all_gather | solution.py:9
  252.9 20.8 %reduce_sum.56 = bf16[2560,1024]{1,0:T(8,128)(2,1)} reduce(bf16[8,2560,1024]{2,1,0:T(8,128)(2,1)} %all-gather.16.cloned.1.call-done, bf16[]{:T(256)} %constant.55.clone.1), dimensions={0}, to_apply=%region_4.5 | reduce | flops 18350080 | bytes 47185920 | tf_op jit(solution)/shard_map/reduce_sum | solution.py:9
  273.8 178.1 %all-gather.18.cloned.1.call-done = bf16[8,2560,1024]{2,1,0:T(8,128)(2,1)} async-done(((bf16[1,2560,1024]{2,1,0:T(8,128)(2,1)}), bf16[8,2560,1024]{2,1,0:T(8,128)(2,1)}) %all-gather.18.cloned.1.call-update) | async-done | bytes 41943056 | tf_op jit(solution)/shard_map/all_gather | solution.py:9
  451.9 20.9 %reduce_sum.57 = bf16[2560,1024]{1,0:T(8,128)(2,1)} reduce(bf16[8,2560,1024]{2,1,0:T(8,128)(2,1)} %all-gather.18.cloned.1.call-done, bf16[]{:T(256)} %constant.55.clone.1), dimensions={0}, to_apply=%region_5.6 | reduce | flops 18350080 | bytes 47185920 | tf_op jit(solution)/shard_map/reduce_sum | solution.py:9
  472.8 177.9 %all-gather.20.cloned.1.call-done = bf16[8,1024,2560]{2,1,0:T(8,128)(2,1)} async-done(((bf16[1,1024,2560]{2,1,0:T(8,128)(2,1)}), bf16[8,1024,2560]{2,1,0:T(8,128)(2,1)}) %all-gather.20.cloned.1.call-update) | async-done | bytes 41943056 | tf_op jit(solution)/shard_map/all_gather | solution.py:9
  650.7 18.1 %reduce_sum.58 = bf16[1024,2560]{1,0:T(8,128)(2,1)} reduce(bf16[8,1024,2560]{2,1,0:T(8,128)(2,1)} %all-gather.20.cloned.1.call-done, bf16[]{:T(256)} %constant.55.clone.1), dimensions={0}, to_apply=%region_6.7 | reduce | flops 18350080 | bytes 47185920 | tf_op jit(solution)/shard_map/reduce_sum | solution.py:9
  668.7 3.5 fusion.40
  672.2 0.5 copy-done.1
  672.8 1.0 fusion.21
  673.8 0.3 slice-done
  674.0 0.5 slice-done.1
  674.6 0.9 fusion.11
  675.4 0.2 pad_maximum_fusion
  675.7 1.7 copy.13
  677.4 0.0 reduce-scatter.3.cloned.1.call-start
  677.4 18.3 %all_gather.27 = bf16[128,2560]{1,0:T(8,128)(2,1)S(1)} all-gather(bf16[128,640]{1,0:T(8,128)(2,1)S(1)} %copy-done.2), channel_id=1, replica_groups=mesh['expert'=8,'tensor'=4] {'tensor'}, dimensions={1}, use_global_device_ids=true | all-gather | bytes 819200 | tf_op jit(solution)/shard_map/all_gather | solution.py:33
  695.8 3.3 fusion.39
  699.2 37.0 %all-gather.10.cloned.1.call-done = bf16[2560,1024]{1,0:T(8,128)(2,1)} async-done(((bf16[320,1024]{1,0:T(8,128)(2,1)}), bf16[2560,1024]{1,0:T(8,128)(2,1)}) %all-gather.10.cloned.1.call-update) | async-done | bytes 5242896 | tf_op jit(solution)/shard_map/all_gather | solution.py:51
  736.2 42.9 %all-gather.12.cloned.1.call-done = bf16[1024,2560]{0,1:T(8,128)(2,1)} async-done(((bf16[1024,320]{0,1:T(8,128)(2,1)}), bf16[1024,2560]{0,1:T(8,128)(2,1)}) %all-gather.12.cloned.1.call-update) | async-done | bytes 5242896 | tf_op jit(solution)/shard_map/all_gather | solution.py:57
  779.1 7.8 fusion.26
  786.9 46.8 %reduce-scatter.5.cloned.1.call-done = f32[256,640]{1,0:T(8,128)} async-done(((f32[256,2560]{1,0:T(8,128)}), f32[256,640]{1,0:T(8,128)}) %reduce-scatter.5.cloned.1.call-update) | async-done | bytes 655376 | tf_op jit(solution)/shard_map/reduce_scatter | solution.py:90
  833.7 1.8 convert_element_type.37
  835.5 3.7 all-to-all-start.1
  839.2 0.3 fusion.25
  839.5 27.5 %reduce-scatter.3.cloned.1.call-done = f32[128,640]{1,0:T(8,128)} async-done(((f32[128,2560]{1,0:T(8,128)}), f32[128,640]{1,0:T(8,128)}) %reduce-scatter.3.cloned.1.call-update) | async-done | bytes 327696 | tf_op jit(solution)/shard_map/reduce_scatter | solution.py:60
  866.9 1.9 fusion.24
  (36 shorter events, 0.3 us)
Async XLA Ops:
  6.5 832.6 %copy-start = (bf16[2560,8]{0,1:T(8,128)(2,1)S(1)}, bf16[2560,8]{0,1:T(8,128)(2,1)}, u32[]{:S(2)}) copy-start(bf16[2560,8]{0,1:T(8,128)(2,1)} %param.15) | copy-start | bytes 122884
  6.5 48.1 %all-gather.14.cloned.1.call-start = ((), (), s32[]{:S(2)}) async-start(), calls=%async_computation.8 | async-start | bytes 1638400 | tf_op jit(solution)/shard_map/all_gather | solution.py:71
  22.9 230.1 %all-gather.16.cloned.1.call-start = ((), (), s32[]{:S(2)}) async-start(), calls=%async_computation.9 | async-start | bytes 47185920 | tf_op jit(solution)/shard_map/all_gather | solution.py:9
  26.3 425.6 %all-gather.18.cloned.1.call-start = ((), (), s32[]{:S(2)}) async-start(), calls=%async_computation.10 | async-start | bytes 47185920 | tf_op jit(solution)/shard_map/all_gather | solution.py:9
  29.0 621.7 %all-gather.20.cloned.1.call-start = ((), (), s32[]{:S(2)}) async-start(), calls=%async_computation.11 | async-start | bytes 47185920 | tf_op jit(solution)/shard_map/all_gather | solution.py:9
  31.6 28.1 %slice-start.4 = ((s8[5242880]{0:T(1024)(128)(4,1)}), s8[1048576]{0:T(1024)(128)(4,1)S(1)}, s32[]{:S(2)}) async-start(s8[5242880]{0:T(1024)(128)(4,1)} %bitcast.64), calls=%async_computation.17 | async-start | bytes 2097152
  31.7 664.1 %all-gather.8.cloned.1.call-start = ((), (), s32[]{:S(2)}) async-start(), calls=%async_computation.4 | async-start | bytes 5898240 | tf_op jit(solution)/shard_map/all_gather | solution.py:46
  32.3 703.9 %all-gather.10.cloned.1.call-start = ((), (), s32[]{:S(2)}) async-start(), calls=%async_computation.5 | async-start | bytes 5898240 | tf_op jit(solution)/shard_map/all_gather | solution.py:51
  32.8 746.2 %all-gather.12.cloned.1.call-start = ((), (), s32[]{:S(2)}) async-start(), calls=%async_computation.6 | async-start | bytes 5898240 | tf_op jit(solution)/shard_map/all_gather | solution.py:57
  33.6 800.1 %reduce-scatter.5.cloned.1.call-start = ((), (), s32[]{:S(2)}) async-start(), calls=%async_computation.12 | async-start | bytes 3276800 | tf_op jit(solution)/shard_map/reduce_scatter | solution.py:90
  54.7 5.1 slice-start.5
  56.2 4.6 slice-start.2
  59.8 1.4 slice-start.3
  668.7 4.0 copy-start.1
  668.7 5.3 slice-start
  672.8 1.8 slice-start.1
  675.7 1.8 copy-start.2
  677.4 189.6 %reduce-scatter.3.cloned.1.call-start = ((), (), s32[]{:S(2)}) async-start(), calls=%async_computation.7 | async-start | bytes 1638400 | tf_op jit(solution)/shard_map/reduce_scatter | solution.py:60
  699.1 87.7 %copy-start.3 = (s32[128,1]{0,1:T(1,128)S(1)}, s32[128,1]{0,1:T(1,128)}, u32[]{:S(2)}) copy-start(s32[128,1]{0,1:T(1,128)} %param.12) | copy-start | bytes 1540
  699.1 140.3 %copy-start.4 = (s32[128]{0:T(128)S(1)}, s32[128]{0:T(128)}, u32[]{:S(2)}) copy-start(s32[128]{0:T(128)} %param.13) | copy-start | bytes 1540
  835.5 31.4 %all-to-all-start.1 = ((bf16[8,32,640]{2,1,0:T(8,128)(2,1)}), bf16[8,32,640]{2,1,0:T(8,128)(2,1)S(1)}, u32[]{:S(2)}, u32[]{:S(2)}) async-start(bf16[8,32,640]{2,1,0:T(8,128)(2,1)} %bitcast.18), calls=%async_computation.3 | async-start | bytes 655360 | tf_op jit(solution)/shard_map/all_to_all | solution.py:93
Sparse Core Ops, SparseCore 0:
  23.0 31.6 all-gather.13
  56.6 196.2 all-gather.15
  254.8 196.9 all-gather.17
  453.6 196.9 all-gather.19
  652.4 40.9 all-gather.7
  695.2 40.9 all-gather.9
  738.1 40.9 all-gather.11
  781.4 52.2 reduce-scatter.4
  836.0 30.9 reduce-scatter.2
